TPU v7x, 32 devices: a whole 2x2x4 slice. The times are simulated.
32 devices in a mesh: rows: 8 (over y, x, core), cols: 4 (over z).
Axes of the slice: x: 2, y: 2, z: 4, core: 2. Of those that a mesh axis runs over, the one named last changes fastest.
Arguments:
- density: bfloat16 [640, 640], P('rows', 'cols'), as said below
- occupancy: int32 [5, 5], replicated, may hold values from 0 to 1, as said below
- square_filter: int32 [5, 5], replicated, may hold values 0 or 1
- cube_filter: int32 [5, 5], replicated, may hold values 0 or 1
Outputs:
- purified: float32 [640, 640], P('rows', 'cols')
Inputs may be any that keep to these rules, and one draw needn't show every extreme that they name: density is symmetric. occupancy is symmetric and every diagonal tile is stored.
All inputs are finite; a program needn't handle non-finite values.
Results may differ from a plain program's by a relative error of at most 0.0095.
Values may be sent and summed in bfloat16 or wider, within the bound.
A program may use at most 64 MiB of HBM per device.

v0:
```python
import jax
import jax.numpy as jnp
from jax import lax
from jax.sharding import PartitionSpec as P

TILE = 128


def expand(table, row_start, row_count, col_start, col_count):
    count = table.shape[0]
    tile_ids = jnp.arange(count, dtype=jnp.int32)
    row_tiles = (jnp.arange(row_count, dtype=jnp.int32) + row_start) // TILE
    col_tiles = (jnp.arange(col_count, dtype=jnp.int32) + col_start) // TILE
    row_pick = (row_tiles[:, None] == tile_ids[None, :]).astype(jnp.float32)
    col_pick = (tile_ids[:, None] == col_tiles[None, :]).astype(jnp.float32)
    left = jnp.dot(row_pick, table.astype(jnp.float32), precision=lax.Precision.HIGHEST)
    return jnp.dot(left, col_pick, precision=lax.Precision.HIGHEST)


def over_panel(step, init, occupied):
    return step(init, lax.all_gather(occupied, "rows", axis=0, tiled=True), jnp.int32(0))


def on_device(density, occupancy, square_filter, cube_filter):
    row_count, col_count = density.shape
    row_start = lax.axis_index("rows") * row_count
    col_start = lax.axis_index("cols") * col_count
    stored_mask = expand(occupancy, row_start, row_count, col_start, col_count)
    square_mask = expand(square_filter, row_start, row_count, col_start, col_count)
    cube_mask = expand(cube_filter, row_start, row_count, col_start, col_count)
    occupied = jnp.where(stored_mask > 0.5, density, jnp.zeros_like(density))
    empty = jnp.zeros((row_count, col_count), jnp.float32)
    panel = lax.all_gather(occupied, "cols", axis=1, tiled=True)

    def add_square(total, piece, start):
        return jnp.dot(panel, piece, preferred_element_type=jnp.float32)

    square_total = over_panel(add_square, empty, occupied)
    square = jnp.where(square_mask > 0.5, square_total, 0.0).astype(jnp.bfloat16)
    square_rows = lax.all_gather(square, "cols", axis=1, tiled=True)

    def add_cube(total, piece, start):
        return jnp.dot(square_rows, piece, preferred_element_type=jnp.float32)

    cube_total = over_panel(add_cube, empty, occupied)
    cube = jnp.where(cube_mask > 0.5, cube_total, 0.0)
    return 3.0 * square.astype(jnp.float32) - 2.0 * cube


def solution(mesh):
    placed = (P("rows", "cols"), P(), P(), P())
    return jax.shard_map(
        on_device, mesh=mesh, in_specs=placed, out_specs=P("rows", "cols"), check_vma=False
    )
```

profile of v0, /device:TPU:0, one launch (start us, length us, event | category | flops | bytes accessed | tf_op | source)
XLA Modules:
  0.0 42.6 jit_solution(16775872245500241807)
XLA Ops:
  0.0 0.0 copy-start
  0.0 0.9 %fusion.5 = f32[80,5]{1,0:T(8,128)S(1)} fusion(s32[80]{0:T(128)S(1)} %and_select_fusion.1, s32[5,5]{1,0:T(8,128)} %param.5), kind=kOutput, calls=%fused_computation.11 | convolution fusion | flops 24425 | bytes 2020 | tf_op jit(solution)/shard_map/dot_general | solution.py:16
  0.9 0.0 copy-done
  0.9 0.2 fusion.3
  1.1 0.0 copy-start.1
  1.1 0.1 copy.5
  1.2 0.6 %copy-done.1 = s32[5,5]{1,0:T(8,128)S(1)} copy-done((s32[5,5]{1,0:T(8,128)S(1)}, s32[5,5]{1,0:T(8,128)}, u32[]{:S(2)}) %copy-start.1) | copy-done | bytes 124
  1.8 0.2 fusion.6
  2.0 0.0 copy-start.2
  2.0 0.2 convolution_compare_fusion.2
  2.2 0.5 %copy-done.2 = s32[5,5]{1,0:T(8,128)S(1)} copy-done((s32[5,5]{1,0:T(8,128)S(1)}, s32[5,5]{1,0:T(8,128)}, u32[]{:S(2)}) %copy-start.2) | copy-done | bytes 124
  2.7 0.2 fusion.4
  2.9 0.2 convolution_compare_fusion
  3.1 15.2 %all_gather.10 = bf16[80,640]{0,1:T(8,128)(2,1)S(1)} all-gather(bf16[80,160]{0,1:T(8,128)(2,1)S(1)} %copy.5), channel_id=1, replica_groups=mesh['rows'=8,'cols'=4] {'cols'}, dimensions={1}, use_global_device_ids=true | all-gather | bytes 128000 | tf_op jit(solution)/shard_map/all_gather | solution.py:33
  18.3 9.4 %all_gather.11 = bf16[640,160]{1,0:T(8,128)(2,1)S(1)} all-gather(bf16[80,160]{1,0:T(8,128)(2,1)S(1)} %fusion.3), channel_id=1, replica_groups=mesh['rows'=8,'cols'=4] {'rows'}, dimensions={0}, use_global_device_ids=true | all-gather | bytes 230400 | tf_op jit(solution)/shard_map/all_gather | solution.py:21
  27.7 0.2 fusion.2
  27.9 0.1 copy.6
  28.0 13.7 %all_gather.12 = bf16[80,640]{0,1:T(8,128)(2,1)S(1)} all-gather(bf16[80,160]{0,1:T(8,128)(2,1)S(1)} %copy.6), channel_id=1, replica_groups=mesh['rows'=8,'cols'=4] {'cols'}, dimensions={1}, use_global_device_ids=true | all-gather | bytes 128000 | tf_op jit(solution)/shard_map/all_gather | solution.py:40
  41.7 0.9 %fusion.1 = f32[80,160]{1,0:T(8,128)} fusion(pred[80,160]{1,0:T(8,128)(4,1)S(1)} %convolution_compare_fusion, bf16[80,640]{0,1:T(8,128)(2,1)S(1)} %all_gather.12, bf16[640,160]{1,0:T(8,128)(2,1)S(1)} %all_gather.11, bf16[80,160]{1,0:T(8,128)(2,1)S(1)} %fusion.2), kind=kOutput, calls=%fused_computation.3 | convolution fusion | flops 16448000 | bytes 396800 | tf_op jit(solution)/shard_map/dot_general | solution.py:43
  (2 shorter events, 0.0 us)
Async XLA Ops:
  0.0 0.9 %copy-start = (bf16[80,160]{1,0:T(8,128)(2,1)S(1)}, bf16[80,160]{1,0:T(8,128)(2,1)}, u32[]{:S(2)}) copy-start(bf16[80,160]{1,0:T(8,128)(2,1)} %param.4) | copy-start | bytes 76804
  1.1 0.7 %copy-start.1 = (s32[5,5]{1,0:T(8,128)S(1)}, s32[5,5]{1,0:T(8,128)}, u32[]{:S(2)}) copy-start(s32[5,5]{1,0:T(8,128)} %param.6) | copy-start | bytes 304
  2.0 0.7 %copy-start.2 = (s32[5,5]{1,0:T(8,128)S(1)}, s32[5,5]{1,0:T(8,128)}, u32[]{:S(2)}) copy-start(s32[5,5]{1,0:T(8,128)} %param.7) | copy-start | bytes 304
where the time goes:
time: 42.9 us; the launch traced here: 42.6 us
  blocking collectives  38.3 us (89%)
  matrix products  2.92 us (7%)
  local copies, waits for them, and re-layouts  1.3 us (3%)
    all_gather x1, blocking collectives, on_device(): panel = lax.all_gather(occupied, 'cols', axis=1, tiled=True)  15.2 us
    all_gather x1, blocking collectives, on_device(): square_rows = lax.all_gather(square, 'cols', axis=1, tiled=True)  13.7 us
    all_gather x1, blocking collectives, over_panel(): lax.all_gather(occupied, 'rows', axis=0, tiled=True)  9.43 us
    dot_general x3, matrix products, expand(): jnp.dot(row_pick, table.astype(jnp.float32), precision=lax.Precision.HIGH...  1.33 us
    unnamed x6, local copies, waits for them, and re-layouts  1.08 us
    dot_general x1, matrix products, add_cube(): return jnp.dot(square_rows, piece, preferred_element_type=jnp.float32)  0.86 us

commit v1 on v0

v1 whole, which is shorter than its diff:
```python
import functools

import jax
import jax.numpy as jnp
from jax import lax
from jax.experimental import pallas as pl
from jax.experimental.pallas import tpu as pltpu
from jax.sharding import PartitionSpec as P

TILE = 128
MESH = pl.DeviceIdType.MESH


def tiles_touched(blocks, size):
    return max(((b + 1) * size - 1) // TILE - b * size // TILE + 1 for b in range(blocks))


def mask_of(table, r, c, nr, nc, h, w):
    last = table.shape[0] - 1
    row_start, col_start = r * h, c * w
    row_tile, col_tile = row_start // TILE, col_start // TILE
    rows = row_start - row_tile * TILE + lax.broadcasted_iota(jnp.int32, (h, w), 0)
    cols = col_start - col_tile * TILE + lax.broadcasted_iota(jnp.int32, (h, w), 1)
    row_tiles, col_tiles = tiles_touched(nr, h), tiles_touched(nc, w)

    def row_values(i):
        tile = jnp.minimum(row_tile + i, last)
        value = jnp.full((h, w), table[tile, jnp.minimum(col_tile + col_tiles - 1, last)], jnp.int32)
        for j in range(col_tiles - 2, -1, -1):
            value = jnp.where(cols < (j + 1) * TILE, table[tile, col_tile + j], value)
        return value

    value = row_values(row_tiles - 1)
    for i in range(row_tiles - 2, -1, -1):
        value = jnp.where(rows < (i + 1) * TILE, row_values(i), value)
    return value > 0


def kernel(
    nr, nc, density, occupancy, square_filter, cube_filter, out,
    own, square, panel, column, squares,
    row_send, row_recv, col_send, col_recv, sq_send, sq_recv,
):
    r, c = lax.axis_index("rows"), lax.axis_index("cols")
    h, w = density.shape
    per = nr // nc

    barrier = pltpu.get_barrier_semaphore()
    row_peers = [lax.rem(c + d, nc) for d in range(1, nc)]
    col_peers = [lax.rem(r + d, nr) for d in range(1, nr)]
    for p in row_peers:
        pl.semaphore_signal(barrier, inc=1, device_id=(r, p), device_id_type=MESH)
    for p in col_peers:
        pl.semaphore_signal(barrier, inc=1, device_id=(p, c), device_id_type=MESH)

    stored = mask_of(occupancy, r, c, nr, nc, h, w)
    mine = jnp.where(stored, density[...].astype(jnp.float32), 0.0).astype(jnp.bfloat16)
    own[...] = mine
    panel[c] = mine
    column[r] = mine
    square_mask = mask_of(square_filter, r, c, nr, nc, h, w)

    pl.semaphore_wait(barrier, nr + nc - 2)

    sends = []
    for d, p in enumerate(row_peers):
        sends.append(pltpu.make_async_remote_copy(
            own, panel.at[c], row_send.at[d], row_recv.at[d], device_id=(r, p), device_id_type=MESH))
    for d, p in enumerate(col_peers):
        sends.append(pltpu.make_async_remote_copy(
            own, column.at[r], col_send.at[d], col_recv.at[d], device_id=(p, c), device_id_type=MESH))
    for s in sends:
        s.start()
    for d in range(nc - 1):
        src = lax.rem(c + nc - 1 - d, nc)
        pltpu.make_async_remote_copy(
            own, panel.at[src], row_send.at[d], row_recv.at[d], device_id=(r, src), device_id_type=MESH).wait_recv()
    for d in range(nr - 1):
        src = lax.rem(r + nr - 1 - d, nr)
        pltpu.make_async_remote_copy(
            own, column.at[src], col_send.at[d], col_recv.at[d], device_id=(src, c), device_id_type=MESH).wait_recv()

    def columns_at(k):
        return column[pl.ds(k * per, per)].reshape(per * h, w)

    total = jnp.zeros((h, w), jnp.float32)
    for k in range(nc):
        total += jnp.dot(panel[k], columns_at(k), preferred_element_type=jnp.float32)
    mine2 = jnp.where(square_mask, total, 0.0).astype(jnp.bfloat16)
    square[...] = mine2
    sq = []
    for d, p in enumerate(row_peers):
        sq.append(pltpu.make_async_remote_copy(
            square, squares.at[d], sq_send.at[d], sq_recv.at[d], device_id=(r, p), device_id_type=MESH))
    for s in sq:
        s.start()
    cube = jnp.dot(mine2, columns_at(c), preferred_element_type=jnp.float32)
    cube_mask = mask_of(cube_filter, r, c, nr, nc, h, w)
    for d in range(nc - 1):
        src = lax.rem(c + nc - 1 - d, nc)
        sq[d].wait_recv()
        cube += jnp.dot(squares[d], columns_at(src), preferred_element_type=jnp.float32)
    out[...] = 3.0 * mine2.astype(jnp.float32) - 2.0 * jnp.where(cube_mask, cube, 0.0)
    for s in sends + sq:
        s.wait_send()


def solution(mesh):
    nr, nc = mesh.shape["rows"], mesh.shape["cols"]

    def step(density, occupancy, square_filter, cube_filter):
        h, w = density.shape
        bf = jnp.bfloat16
        return pl.pallas_call(
            functools.partial(kernel, nr, nc),
            out_shape=jax.ShapeDtypeStruct((h, w), jnp.float32),
            in_specs=[pl.BlockSpec(memory_space=pltpu.VMEM)]
            + [pl.BlockSpec(memory_space=pltpu.SMEM)] * 3,
            out_specs=pl.BlockSpec(memory_space=pltpu.VMEM),
            scratch_shapes=[
                pltpu.VMEM((h, w), bf),
                pltpu.VMEM((h, w), bf),
                pltpu.VMEM((nc, h, w), bf),
                pltpu.VMEM((nr, h, w), bf),
                pltpu.VMEM((nc - 1, h, w), bf),
                pltpu.SemaphoreType.DMA((nc - 1,)),
                pltpu.SemaphoreType.DMA((nc - 1,)),
                pltpu.SemaphoreType.DMA((nr - 1,)),
                pltpu.SemaphoreType.DMA((nr - 1,)),
                pltpu.SemaphoreType.DMA((nc - 1,)),
                pltpu.SemaphoreType.DMA((nc - 1,)),
            ],
            compiler_params=pltpu.CompilerParams(collective_id=0, has_side_effects=True),
        )(density, occupancy, square_filter, cube_filter)

    placed = (P("rows", "cols"), P(), P(), P())
    return jax.shard_map(
        step, mesh=mesh, in_specs=placed, out_specs=P("rows", "cols"), check_vma=False
    )
```

time: 42.9 us -> 19.8 us (0.46)
  blocking collectives: 38.3 us -> 0 us
  Pallas kernels: 0 us -> 18 us
  matrix products: 2.92 us -> 0 us
    all_gather x3 -> x0, blocking collectives: 38.3 us -> none  [the longest x1 15.2 us: on_device(): panel = lax.all_gather(occupied, 'cols', axis=1, tiled=True)]
    pallas_call x0 -> x1, Pallas kernels: none -> 18 us  [step(): pl.pallas_call(functools.partial(kernel, nr, nc), out_shape=jax.ShapeDtyp...]
    dot_general x8 -> x0, matrix products: 2.92 us -> none  [the longest x3 1.33 us: expand(): jnp.dot(row_pick, table.astype(jnp.float32), precision=lax.Precision.HIGH...]
    unnamed x6 -> x1, local copies, waits for them, and re-layouts: 1.08 us -> 1.53 us
where the time goes in v1:
time: 19.8 us; the launch traced here: 19.5 us
  Pallas kernels  18 us (91%)
  local copies, waits for them, and re-layouts  1.53 us (8%)
    pallas_call x1, Pallas kernels, step(): pl.pallas_call(functools.partial(kernel, nr, nc), out_shape=jax.ShapeDtyp...  18 us
    unnamed x1, local copies, waits for them, and re-layouts  1.53 us

profile of v1, /device:TPU:0, one launch (start us, length us, event | category | flops | bytes accessed | tf_op | source)
XLA Modules:
  0.0 19.5 jit_solution(12126089338748077728)
XLA Ops:
  0.0 18.0 %shard_map.46 = f32[80,160]{1,0:T(8,128)} custom-call(bf16[80,160]{1,0:T(8,128)(2,1)} %density.1, s32[5,5]{1,0:T(8,128)} %occupancy.1, s32[5,5]{1,0:T(8,128)} %square_filter.1, s32[5,5]{1,0:T(8,128)} %cube_filter.1), custom_call_target="tpu_custom_call" | custom-call | tf_op jit(solution)/shard_map/pallas_call | solution.py:114
  18.0 1.5 %copy.6 = f32[80,160]{1,0:T(8,128)} copy(f32[80,160]{1,0:T(8,128)} %shard_map.46) | data formatting | bytes 102400
